TPU v7x, 32 devices: a whole 2x2x4 slice. The times are simulated.
32 devices in a mesh: member: 16 (over z, y, core), slab: 2 (over x).
Axes of the slice: x: 2, y: 2, z: 4, core: 2. Of those that a mesh axis runs over, the one named last changes fastest.
Arguments:
- checkpoint: float32 [16, 2, 4, 256, 256], P('member', None, 'slab'), may hold values from 0 to 1
- adjoint_late: float32 [16, 2, 4, 256, 256], P('member', None, 'slab'), may hold values from -6 to 6
- rate_params: float32 [64, 64], replicated, may hold values from 0.02 to 0.1
- perturbation: float32 [16, 64, 64], P('member'), may hold values from -0.5 to 0.5
Outputs:
- adjoint_early: float32 [16, 2, 4, 256, 256], P('member', None, 'slab')
- param_grad: float32 [64, 64], replicated
All inputs are finite; a program needn't handle non-finite values.
Results may differ from a plain program's by a relative error of at most 0.00002.
Values sent between devices are 32-bit elements; how exact they have to be, the bound alone decides.
A program may use at most 64 MiB of HBM per device.

v0:
```python
import jax
import jax.numpy as jnp
from jax import lax
from jax.sharding import PartitionSpec as P

PX = 64
PY = 64
SX = 4
SY = 4
NX = 256
NY = 256
feed_rate = 0.035
substrate_diffusion = 0.16
activator_diffusion = 0.08


def with_halo(cells, sides, width):
    for axis, dim in sides:
        count = lax.axis_size(axis)
        ends = count - 1
        head = lax.slice_in_dim(cells, 0, width, axis=dim)
        tail = lax.slice_in_dim(cells, cells.shape[dim] - width, cells.shape[dim], axis=dim)
        cells = jnp.concatenate(
            [
                lax.ppermute(tail, axis, [(i, (i + 1) % count) for i in range(ends)]),
                cells,
                lax.ppermute(head, axis, [((i + 1) % count, i) for i in range(ends)]),
            ],
            axis=dim,
        )
    return cells


def laplace_rim(extended):
    padded = jnp.pad(extended, ((0, 0), (0, 0), (1, 1), (1, 1)))
    center = padded[:, 1:-1, 1:-1, 1:-1]
    summed = padded[:, 2:, 1:-1, 1:-1] + padded[:, :-2, 1:-1, 1:-1]
    summed = summed + padded[:, 1:-1, 2:, 1:-1] + padded[:, 1:-1, :-2, 1:-1]
    summed = summed + padded[:, 1:-1, 1:-1, 2:] + padded[:, 1:-1, 1:-1, :-2]
    return summed - 6.0 * center


def advance(extended, decay_rate):
    laplace = laplace_rim(extended)
    u_field = extended[0, 1:-1]
    v_field = extended[1, 1:-1]
    reaction = u_field * v_field * v_field
    u_new = u_field + substrate_diffusion * laplace[0] - reaction + feed_rate * (1.0 - u_field)
    v_new = (
        v_field + activator_diffusion * laplace[1] + reaction - (feed_rate + decay_rate) * v_field
    )
    return jnp.stack([u_new, v_new])


def pull_back(status, adjoint_ext, decay_rate):
    laplace = laplace_rim(adjoint_ext)
    adj_u = adjoint_ext[0, 1:-1]
    adj_v = adjoint_ext[1, 1:-1]
    uv_prod = status[0] * status[1]
    v_square = status[1] * status[1]
    new_u = (
        adj_u + substrate_diffusion * laplace[0] - (v_square + feed_rate) * adj_u + v_square * adj_v
    )
    new_v = (
        adj_v
        + activator_diffusion * laplace[1]
        - 2.0 * uv_prod * adj_u
        + (2.0 * uv_prod - feed_rate - decay_rate) * adj_v
    )
    return jnp.stack([new_u, new_v])


def expand_params(table):
    return jnp.broadcast_to(table[:, None, :, None], (PX, SX, PY, SY)).reshape(NX, NY)


def patch_total(field):
    return jnp.sum(field.reshape(PX, SX, PY, SY), axis=(1, 3))


def local(checkpoint, adjoint_late, rate_params, perturbation):
    start_state = checkpoint[0]
    adjoint_two = adjoint_late[0]
    factor = 1.0 + perturbation[0]
    decay_rate = expand_params(rate_params * factor)
    member_count = lax.axis_size("member")
    state_ext, adjoint_ext_two = (
        with_halo(start_state, (("slab", 1),), 1),
        with_halo(adjoint_two, (("slab", 1),), 1),
    )
    middle = advance(state_ext, decay_rate)
    adjoint_one = pull_back(middle, adjoint_ext_two, decay_rate)
    first_term = -jnp.sum(middle[1] * adjoint_two[1], 0)
    adjoint_ext = with_halo(adjoint_one, (("slab", 1),), 1)
    adjoint_zero = pull_back(start_state, adjoint_ext, decay_rate)
    second = -jnp.sum(start_state[1] * adjoint_one[1], 0)
    param_grad = (
        lax.psum(patch_total(first_term + second) * factor, ("member", "slab")) / member_count
    )
    return (adjoint_zero[None], param_grad)


def solution(mesh):
    return jax.shard_map(
        local,
        mesh=mesh,
        in_specs=(
            P("member", None, "slab", None, None),
            P("member", None, "slab", None, None),
            P(),
            P("member", None, None),
        ),
        out_specs=(P("member", None, "slab", None, None), P()),
        check_vma=False,
    )
```

profile of v0, /device:TPU:0, one launch (start us, length us, event | category | flops | bytes accessed | tf_op | source)
XLA Modules:
  0.0 109.7 jit_solution(6081477376851431871)
XLA Ops:
  0.6 2.3 %fusion.44 = (f32[2,1,256,256]{3,2,1,0:T(8,128)}, f32[2,1,256,256]{3,2,1,0:T(8,128)}) fusion(f32[2,2,256,256]{3,2,1,0:T(8,128)} %bitcast.149), kind=kLoop, calls=%fused_computation.112 | loop fusion | bytes 2097152 | tf_op jit(solution)/shard_map/slice | solution.py:22
  2.9 1.3 %collective-permute-start = (f32[2,1,256,256]{3,2,1,0:T(8,128)}, f32[2,1,256,256]{3,2,1,0:T(8,128)S(1)}, u32[]{:S(2)}, u32[]{:S(2)}) collective-permute-start(f32[2,1,256,256]{3,2,1,0:T(8,128)} %get-tuple-element.13), channel_id=1, source_target_pairs={{1,0},{3,2},{5,4},{7,6},{9,8},{11,10},{13,12},{15,14},{17,16},{19,... | collective-permute-start | bytes 1572872 | tf_op jit(solution)/shard_map/ppermute | solution.py:27
  4.2 4.9 %collective-permute-start.1 = (f32[2,1,256,256]{3,2,1,0:T(8,128)}, f32[2,1,256,256]{3,2,1,0:T(8,128)S(1)}, u32[]{:S(2)}, u32[]{:S(2)}) collective-permute-start(f32[2,1,256,256]{3,2,1,0:T(8,128)} %get-tuple-element.12), channel_id=1, source_target_pairs={{0,1},{2,3},{4,5},{6,7},{8,9},{10,11},{12,13},{14,15},{16,17},{18,... | collective-permute-start | bytes 1572872 | tf_op jit(solution)/shard_map/ppermute | solution.py:25
  9.1 2.4 %fusion.43 = (f32[2,1,256,256]{3,2,1,0:T(8,128)}, f32[2,1,256,256]{3,2,1,0:T(8,128)}) fusion(f32[2,2,256,256]{3,2,1,0:T(8,128)} %bitcast.146), kind=kLoop, calls=%fused_computation.111 | loop fusion | bytes 2097152 | tf_op jit(solution)/shard_map/slice | solution.py:22
  11.5 1.3 %collective-permute-start.2 = (f32[2,1,256,256]{3,2,1,0:T(8,128)}, f32[2,1,256,256]{3,2,1,0:T(8,128)S(1)}, u32[]{:S(2)}, u32[]{:S(2)}) collective-permute-start(f32[2,1,256,256]{3,2,1,0:T(8,128)} %get-tuple-element.11), channel_id=1, source_target_pairs={{1,0},{3,2},{5,4},{7,6},{9,8},{11,10},{13,12},{15,14},{17,16},{19,... | collective-permute-start | bytes 1572872 | tf_op jit(solution)/shard_map/ppermute | solution.py:27
  12.8 5.4 %collective-permute-start.3 = (f32[2,1,256,256]{3,2,1,0:T(8,128)}, f32[2,1,256,256]{3,2,1,0:T(8,128)}, u32[]{:S(2)}, u32[]{:S(2)}) collective-permute-start(f32[2,1,256,256]{3,2,1,0:T(8,128)} %get-tuple-element.10), channel_id=1, source_target_pairs={{0,1},{2,3},{4,5},{6,7},{8,9},{10,11},{12,13},{14,15},{16,17},{18,... | collective-permute-start | bytes 1572872 | tf_op jit(solution)/shard_map/ppermute | solution.py:25
  18.2 3.8 %broadcast_in_dim.4 = f32[64,4,64,4]{3,2,1,0:T(8,128)} broadcast(f32[64,64]{1,0:T(8,128)S(1)} %bitcast_multiply_fusion.13), dimensions={0,2} | broadcast | bytes 278528 | tf_op jit(solution)/shard_map/broadcast_in_dim | solution.py:74
  22.0 8.4 %reshape.133 = f32[256,256]{1,0:T(8,128)S(1)} reshape(f32[64,4,64,4]{3,2,1,0:T(8,128)} %broadcast_in_dim.4) | data formatting | bytes 524288 | tf_op jit(solution)/shard_map/reshape | solution.py:74
  30.4 0.0 collective-permute-done
  30.5 0.8 copy-done.2
  31.2 0.8 copy-done.3
  32.0 1.4 %select_maximum_fusion.5 = f32[2,4,258,258]{3,2,1,0:T(8,128)S(1)} fusion(f32[2,1,256,256]{3,2,1,0:T(8,128)S(1)} %collective-permute-done, f32[2,2,256,256]{3,2,1,0:T(8,128)S(1)} %bitcast.150, f32[2,1,256,256]{3,2,1,0:T(8,128)S(1)} %collective-permute-done.1), kind=kLoop, calls=%fused_computation.9 | loop fusion | flops 7987680 | bytes 4227200 | tf_op jit(solution)/shard_map/concatenate | solution.py:23
  33.5 0.0 copy-start
  33.5 2.2 %fusion.8 = f32[2,2,256,256]{3,2,1,0:T(8,128)S(1)} fusion(f32[2,4,258,258]{3,2,1,0:T(8,128)S(1)} %select_maximum_fusion.5, f32[2,2,256,256]{3,2,1,0:T(8,128)S(1)} %bitcast.151, f32[2,1,256,256]{3,2,1,0:T(8,128)} %copy-done.3, f32[2,1,256,256]{3,2,1,0:T(8,128)} %copy-done.2), kind=kLoop, calls=%fused_computation.39 | loop fusion | flops 2359296 | bytes 7340032 | tf_op jit(solution)/shard_map/sub | solution.py:40
  35.7 0.0 collective-permute-done.2
  35.7 2.4 %select_maximum_fusion.3 = f32[2,4,258,258]{3,2,1,0:T(8,128)S(1)} fusion(f32[2,1,256,256]{3,2,1,0:T(8,128)S(1)} %collective-permute-done.2, f32[2,2,256,256]{3,2,1,0:T(8,128)S(1)} %bitcast.147, f32[2,1,256,256]{3,2,1,0:T(8,128)} %collective-permute-done.3), kind=kLoop, calls=%fused_computation.7 | loop fusion | flops 7987680 | bytes 4227200 | tf_op jit(solution)/shard_map/concatenate | solution.py:23
  38.2 2.0 %fusion.6 = f32[2,2,256,256]{3,2,1,0:T(8,128)S(1)} fusion(f32[2,4,258,258]{3,2,1,0:T(8,128)S(1)} %select_maximum_fusion.3, f32[2,2,256,256]{3,2,1,0:T(8,128)S(1)} %bitcast.148, f32[2,1,256,256]{3,2,1,0:T(8,128)} %collective-permute-done.3, f32[2,1,256,256]{3,2,1,0:T(8,128)S(1)} %collective-permute-done.2), kind=kLoop, calls=%fused_computation.31 | loop fusion | flops 2359296 | bytes 7340032 | tf_op jit(solution)/shard_map/sub | solution.py:40
  40.2 0.3 fusion.20
  40.4 0.5 fusion.29
  40.9 0.4 fusion.34
  41.3 1.1 fusion.11
  42.4 1.3 %collective-permute-start.4 = (f32[2,1,256,256]{3,2,1,0:T(8,128)}, f32[2,1,256,256]{3,2,1,0:T(8,128)S(1)}, u32[]{:S(2)}, u32[]{:S(2)}) collective-permute-start(f32[2,1,256,256]{3,2,1,0:T(8,128)} %get-tuple-element.9), channel_id=1, source_target_pairs={{1,0},{3,2},{5,4},{7,6},{9,8},{11,10},{13,12},{15,14},{17,16},{19,... | collective-permute-start | bytes 1572872 | tf_op jit(solution)/shard_map/ppermute | solution.py:27
  43.7 4.6 %collective-permute-start.5 = (f32[2,1,256,256]{3,2,1,0:T(8,128)}, f32[2,1,256,256]{3,2,1,0:T(8,128)S(1)}, u32[]{:S(2)}, u32[]{:S(2)}) collective-permute-start(f32[2,1,256,256]{3,2,1,0:T(8,128)} %get-tuple-element.8), channel_id=1, source_target_pairs={{0,1},{2,3},{4,5},{6,7},{8,9},{10,11},{12,13},{14,15},{16,17},{18,... | collective-permute-start | bytes 1572872 | tf_op jit(solution)/shard_map/ppermute | solution.py:25
  48.3 0.8 negate_add_fusion
  49.0 10.8 %add.226 = f32[64,4,64,4]{3,2,1,0:T(8,128)} reshape(f32[256,256]{1,0:T(8,128)} %negate_add_fusion) | data formatting | bytes 524288 | tf_op jit(solution)/shard_map/add | solution.py:98
  59.9 4.0 %reduce_sum.29 = f32[64,64]{1,0:T(8,128)S(1)} reduce(f32[64,4,64,4]{3,2,1,0:T(8,128)} %add.226, f32[]{:T(128)} %constant.9.clone.1), dimensions={1,3}, to_apply=%region_2.3 | reduce | flops 61440 | bytes 278532 | tf_op jit(solution)/shard_map/reduce_sum | solution.py:78
  63.9 41.0 %psum.7 = f32[64,64]{1,0:T(8,128)S(1)} all-reduce(f32[64,64]{1,0:T(8,128)S(1)} %bitcast_multiply_fusion.12), channel_id=1, replica_groups=mesh['member'=16,'slab'=2] {'member','slab'}, use_global_device_ids=true, to_apply=%region_3.4 | all-reduce | flops 4096 | bytes 32768 | tf_op jit(solution)/shard_map/psum | solution.py:98
  104.9 0.6 broadcast_multiply_fusion
  105.5 1.9 %select_maximum_fusion = f32[2,4,258,258]{3,2,1,0:T(8,128)S(1)} fusion(f32[2,1,256,256]{3,2,1,0:T(8,128)S(1)} %collective-permute-done.4, f32[2,1,256,256]{3,2,1,0:T(8,128)S(1)} %collective-permute-done.5, f32[1,2,256,256]{3,2,1,0:T(8,128)S(1)} %fusion.34, f32[1,2,256,256]{3,2,1,0:T(8,128)S(1)} %get-tuple-element.4), kind=kLoop, calls=%fused_computation.4 | loop fusion | flops 9585216 | bytes 4227200 | tf_op jit(solution)/shard_map/concatenate | solution.py:23
  107.4 0.9 fusion.4
  108.4 0.3 fusion.17
  108.7 1.0 maximum_bitcast_fusion
  (16 shorter events, 0.1 us)
Async XLA Ops:
  0.6 17.5 %copy-start.5 = (f32[64,64]{1,0:T(8,128)S(1)}, f32[64,64]{1,0:T(8,128)}, u32[]{:S(2)}) copy-start(f32[64,64]{1,0:T(8,128)} %param.6) | copy-start | bytes 49156
  0.6 17.5 %copy-start.4 = (f32[1,64,64]{2,1,0:T(8,128)S(1)}, f32[1,64,64]{2,1,0:T(8,128)}, u32[]{:S(2)}) copy-start(f32[1,64,64]{2,1,0:T(8,128)} %param.7) | copy-start | bytes 49156
  2.9 27.5 %collective-permute-start = (f32[2,1,256,256]{3,2,1,0:T(8,128)}, f32[2,1,256,256]{3,2,1,0:T(8,128)S(1)}, u32[]{:S(2)}, u32[]{:S(2)}) collective-permute-start(f32[2,1,256,256]{3,2,1,0:T(8,128)} %get-tuple-element.13), channel_id=1, source_target_pairs={{1,0},{3,2},{5,4},{7,6},{9,8},{11,10},{13,12},{15,14},{17,16},{19,... | collective-permute-start | bytes 1572872 | tf_op jit(solution)/shard_map/ppermute | solution.py:27
  4.2 26.3 %collective-permute-start.1 = (f32[2,1,256,256]{3,2,1,0:T(8,128)}, f32[2,1,256,256]{3,2,1,0:T(8,128)S(1)}, u32[]{:S(2)}, u32[]{:S(2)}) collective-permute-start(f32[2,1,256,256]{3,2,1,0:T(8,128)} %get-tuple-element.12), channel_id=1, source_target_pairs={{0,1},{2,3},{4,5},{6,7},{8,9},{10,11},{12,13},{14,15},{16,17},{18,... | collective-permute-start | bytes 1572872 | tf_op jit(solution)/shard_map/ppermute | solution.py:25
  11.5 24.2 %collective-permute-start.2 = (f32[2,1,256,256]{3,2,1,0:T(8,128)}, f32[2,1,256,256]{3,2,1,0:T(8,128)S(1)}, u32[]{:S(2)}, u32[]{:S(2)}) collective-permute-start(f32[2,1,256,256]{3,2,1,0:T(8,128)} %get-tuple-element.11), channel_id=1, source_target_pairs={{1,0},{3,2},{5,4},{7,6},{9,8},{11,10},{13,12},{15,14},{17,16},{19,... | collective-permute-start | bytes 1572872 | tf_op jit(solution)/shard_map/ppermute | solution.py:27
  12.8 23.0 %collective-permute-start.3 = (f32[2,1,256,256]{3,2,1,0:T(8,128)}, f32[2,1,256,256]{3,2,1,0:T(8,128)}, u32[]{:S(2)}, u32[]{:S(2)}) collective-permute-start(f32[2,1,256,256]{3,2,1,0:T(8,128)} %get-tuple-element.10), channel_id=1, source_target_pairs={{0,1},{2,3},{4,5},{6,7},{8,9},{10,11},{12,13},{14,15},{16,17},{18,... | collective-permute-start | bytes 1572872 | tf_op jit(solution)/shard_map/ppermute | solution.py:25
  22.0 10.0 %copy-start.1 = (f32[1,2,2,256,256]{4,3,2,1,0:T(8,128)S(1)}, f32[1,2,2,256,256]{4,3,2,1,0:T(8,128)}, u32[]{:S(2)}) copy-start(f32[1,2,2,256,256]{4,3,2,1,0:T(8,128)} %param.5) | copy-start | bytes 3145732
  30.4 0.8 copy-start.2
  31.2 0.8 copy-start.3
  33.5 2.3 %copy-start = (f32[1,2,2,256,256]{4,3,2,1,0:T(8,128)S(1)}, f32[1,2,2,256,256]{4,3,2,1,0:T(8,128)}, u32[]{:S(2)}) copy-start(f32[1,2,2,256,256]{4,3,2,1,0:T(8,128)} %param.4) | copy-start | bytes 3145732
  42.4 63.2 %collective-permute-start.4 = (f32[2,1,256,256]{3,2,1,0:T(8,128)}, f32[2,1,256,256]{3,2,1,0:T(8,128)S(1)}, u32[]{:S(2)}, u32[]{:S(2)}) collective-permute-start(f32[2,1,256,256]{3,2,1,0:T(8,128)} %get-tuple-element.9), channel_id=1, source_target_pairs={{1,0},{3,2},{5,4},{7,6},{9,8},{11,10},{13,12},{15,14},{17,16},{19,... | collective-permute-start | bytes 1572872 | tf_op jit(solution)/shard_map/ppermute | solution.py:27
  43.7 61.9 %collective-permute-start.5 = (f32[2,1,256,256]{3,2,1,0:T(8,128)}, f32[2,1,256,256]{3,2,1,0:T(8,128)S(1)}, u32[]{:S(2)}, u32[]{:S(2)}) collective-permute-start(f32[2,1,256,256]{3,2,1,0:T(8,128)} %get-tuple-element.8), channel_id=1, source_target_pairs={{0,1},{2,3},{4,5},{6,7},{8,9},{10,11},{12,13},{14,15},{16,17},{18,... | collective-permute-start | bytes 1572872 | tf_op jit(solution)/shard_map/ppermute | solution.py:25
where the time goes:
time: 110 us
  blocking collectives  41 us (37%)
  local copies, waits for them, and re-layouts  29.3 us (27%)
  other arithmetic  19.8 us (18%)
  starting transfers between devices  18.8 us (17%)
    psum x1, blocking collectives, local(): lax.psum(patch_total(first_term + second) * factor, ('member', 'slab'))  41 us
    ppermute x3, starting transfers between devices, with_halo(): lax.ppermute(tail, axis, [(i, (i + 1) % count) for i in range(ends)])  14.9 us
    add x1, local copies, waits for them, and re-layouts, local(): first_term + second  10.8 us
    reshape x1, local copies, waits for them, and re-layouts, expand_params(): jnp.broadcast_to(table[:, None, :, None], (PX, SX, PY, SY)).reshape(NX, NY)  8.39 us
    concatenate x3, other arithmetic, with_halo(): jnp.concatenate([lax.ppermute(tail, axis, [(i, (i + 1) % count) for i in...  5.74 us
    sub x3, other arithmetic, laplace_rim(): return summed - 6.0 * center  5.14 us
    slice x2, local copies, waits for them, and re-layouts, with_halo(): lax.slice_in_dim(cells, cells.shape[dim] - width, cells.shape[dim], axis=...  4.61 us
    reduce_sum x1, other arithmetic, patch_total(): return jnp.sum(field.reshape(PX, SX, PY, SY), axis=(1, 3))  4.01 us
  transfers between devices with their start and end apart: 6, of which 0 were waited for; matrix products, arithmetic and copies ran while one was open for 31% of the time, Pallas kernels for 0%

commit v1 on v0

--- a/solution.py
+++ b/solution.py
@@ -95,7 +95,8 @@
     adjoint_zero = pull_back(start_state, adjoint_ext, decay_rate)
     second = -jnp.sum(start_state[1] * adjoint_one[1], 0)
     param_grad = (
-        lax.psum(patch_total(first_term + second) * factor, ("member", "slab")) / member_count
+        lax.psum(lax.psum(patch_total(first_term + second) * factor, "slab"), "member")
+        / member_count
     )
     return (adjoint_zero[None], param_grad)
 

time: 110 us -> 135 us (1.23)
  blocking collectives: 41 us -> 66.1 us
    psum x1 -> x2, blocking collectives: 41 us -> 66.1 us  [the longest x1 59.2 us: local(): lax.psum(lax.psum(patch_total(first_term + second) * factor, 'slab'), 'me...]
  transfers between devices with their start and end apart: 6 -> 6, of which waited for: 0 -> 0; matrix products, arithmetic and copies ran while one was open for 31% -> 26% of each run, Pallas kernels for 0% -> 0%
where the time goes in v1:
time: 135 us
  blocking collectives  66.1 us (49%)
  local copies, waits for them, and re-layouts  29.2 us (22%)
  other arithmetic  19.8 us (15%)
  starting transfers between devices  18.7 us (14%)
    psum x1, blocking collectives, local(): lax.psum(lax.psum(patch_total(first_term + second) * factor, 'slab'), 'me...  59.2 us
    ppermute x3, starting transfers between devices, with_halo(): lax.ppermute(tail, axis, [(i, (i + 1) % count) for i in range(ends)])  14.9 us
    add x1, local copies, waits for them, and re-layouts, local(): first_term + second  10.8 us
    reshape x1, local copies, waits for them, and re-layouts, expand_params(): jnp.broadcast_to(table[:, None, :, None], (PX, SX, PY, SY)).reshape(NX, NY)  8.39 us
    psum x1, blocking collectives, local(): lax.psum(patch_total(first_term + second) * factor, 'slab')  6.91 us
    concatenate x3, other arithmetic, with_halo(): jnp.concatenate([lax.ppermute(tail, axis, [(i, (i + 1) % count) for i in...  5.74 us
    sub x3, other arithmetic, laplace_rim(): return summed - 6.0 * center  5.14 us
    slice x2, local copies, waits for them, and re-layouts, with_halo(): lax.slice_in_dim(cells, cells.shape[dim] - width, cells.shape[dim], axis=...  4.61 us
  transfers between devices with their start and end apart: 6, of which 0 were waited for; matrix products, arithmetic and copies ran while one was open for 26% of the time, Pallas kernels for 0%

profile of v1, /device:TPU:0, one launch (start us, length us, event | category | flops | bytes accessed | tf_op | source)
XLA Modules:
  0.0 134.8 jit_solution(4622831404279492078)
XLA Ops:
  0.6 2.3 %fusion.44 = (f32[2,1,256,256]{3,2,1,0:T(8,128)}, f32[2,1,256,256]{3,2,1,0:T(8,128)}) fusion(f32[2,2,256,256]{3,2,1,0:T(8,128)} %bitcast.149), kind=kLoop, calls=%fused_computation.112 | loop fusion | bytes 2097152 | tf_op jit(solution)/shard_map/slice | solution.py:22
  2.9 1.3 collective-permute-start
  4.2 4.9 %collective-permute-start.1 = (f32[2,1,256,256]{3,2,1,0:T(8,128)}, f32[2,1,256,256]{3,2,1,0:T(8,128)S(1)}, u32[]{:S(2)}, u32[]{:S(2)}) collective-permute-start(f32[2,1,256,256]{3,2,1,0:T(8,128)} %get-tuple-element.12), channel_id=1, source_target_pairs={{0,1},{2,3},{4,5},{6,7},{8,9},{10,11},{12,13},{14,15},{16,17},{18,... | collective-permute-start | bytes 1572872 | tf_op jit(solution)/shard_map/ppermute | solution.py:25
  9.1 2.4 %fusion.43 = (f32[2,1,256,256]{3,2,1,0:T(8,128)}, f32[2,1,256,256]{3,2,1,0:T(8,128)}) fusion(f32[2,2,256,256]{3,2,1,0:T(8,128)} %bitcast.146), kind=kLoop, calls=%fused_computation.111 | loop fusion | bytes 2097152 | tf_op jit(solution)/shard_map/slice | solution.py:22
  11.5 1.3 collective-permute-start.2
  12.8 5.4 %collective-permute-start.3 = (f32[2,1,256,256]{3,2,1,0:T(8,128)}, f32[2,1,256,256]{3,2,1,0:T(8,128)}, u32[]{:S(2)}, u32[]{:S(2)}) collective-permute-start(f32[2,1,256,256]{3,2,1,0:T(8,128)} %get-tuple-element.10), channel_id=1, source_target_pairs={{0,1},{2,3},{4,5},{6,7},{8,9},{10,11},{12,13},{14,15},{16,17},{18,... | collective-permute-start | bytes 1572872 | tf_op jit(solution)/shard_map/ppermute | solution.py:25
  18.2 3.8 %broadcast_in_dim.4 = f32[64,4,64,4]{3,2,1,0:T(8,128)} broadcast(f32[64,64]{1,0:T(8,128)S(1)} %bitcast_multiply_fusion.13), dimensions={0,2} | broadcast | bytes 278528 | tf_op jit(solution)/shard_map/broadcast_in_dim | solution.py:74
  22.0 8.4 %reshape.133 = f32[256,256]{1,0:T(8,128)S(1)} reshape(f32[64,4,64,4]{3,2,1,0:T(8,128)} %broadcast_in_dim.4) | data formatting | bytes 524288 | tf_op jit(solution)/shard_map/reshape | solution.py:74
  30.4 0.0 collective-permute-done
  30.4 0.8 copy-done.2
  31.2 0.8 copy-done.3
  32.0 1.4 %select_maximum_fusion.5 = f32[2,4,258,258]{3,2,1,0:T(8,128)S(1)} fusion(f32[2,1,256,256]{3,2,1,0:T(8,128)S(1)} %collective-permute-done, f32[2,2,256,256]{3,2,1,0:T(8,128)S(1)} %bitcast.150, f32[2,1,256,256]{3,2,1,0:T(8,128)S(1)} %collective-permute-done.1), kind=kLoop, calls=%fused_computation.9 | loop fusion | flops 7987680 | bytes 4227200 | tf_op jit(solution)/shard_map/concatenate | solution.py:23
  33.5 0.0 copy-start
  33.5 2.2 %fusion.8 = f32[2,2,256,256]{3,2,1,0:T(8,128)S(1)} fusion(f32[2,4,258,258]{3,2,1,0:T(8,128)S(1)} %select_maximum_fusion.5, f32[2,2,256,256]{3,2,1,0:T(8,128)S(1)} %bitcast.151, f32[2,1,256,256]{3,2,1,0:T(8,128)} %copy-done.3, f32[2,1,256,256]{3,2,1,0:T(8,128)} %copy-done.2), kind=kLoop, calls=%fused_computation.39 | loop fusion | flops 2359296 | bytes 7340032 | tf_op jit(solution)/shard_map/sub | solution.py:40
  35.7 2.4 %select_maximum_fusion.3 = f32[2,4,258,258]{3,2,1,0:T(8,128)S(1)} fusion(f32[2,1,256,256]{3,2,1,0:T(8,128)S(1)} %collective-permute-done.2, f32[2,2,256,256]{3,2,1,0:T(8,128)S(1)} %bitcast.147, f32[2,1,256,256]{3,2,1,0:T(8,128)} %collective-permute-done.3), kind=kLoop, calls=%fused_computation.7 | loop fusion | flops 7987680 | bytes 4227200 | tf_op jit(solution)/shard_map/concatenate | solution.py:23
  38.2 2.0 %fusion.6 = f32[2,2,256,256]{3,2,1,0:T(8,128)S(1)} fusion(f32[2,4,258,258]{3,2,1,0:T(8,128)S(1)} %select_maximum_fusion.3, f32[2,2,256,256]{3,2,1,0:T(8,128)S(1)} %bitcast.148, f32[2,1,256,256]{3,2,1,0:T(8,128)} %collective-permute-done.3, f32[2,1,256,256]{3,2,1,0:T(8,128)S(1)} %collective-permute-done.2), kind=kLoop, calls=%fused_computation.31 | loop fusion | flops 2359296 | bytes 7340032 | tf_op jit(solution)/shard_map/sub | solution.py:40
  40.2 0.3 fusion.20
  40.4 0.5 fusion.29
  40.9 0.4 fusion.34
  41.3 1.1 fusion.11
  42.3 1.3 collective-permute-start.4
  43.6 4.6 %collective-permute-start.5 = (f32[2,1,256,256]{3,2,1,0:T(8,128)}, f32[2,1,256,256]{3,2,1,0:T(8,128)S(1)}, u32[]{:S(2)}, u32[]{:S(2)}) collective-permute-start(f32[2,1,256,256]{3,2,1,0:T(8,128)} %get-tuple-element.8), channel_id=1, source_target_pairs={{0,1},{2,3},{4,5},{6,7},{8,9},{10,11},{12,13},{14,15},{16,17},{18,... | collective-permute-start | bytes 1572872 | tf_op jit(solution)/shard_map/ppermute | solution.py:25
  48.3 0.8 negate_add_fusion
  49.0 10.8 %add.228 = f32[64,4,64,4]{3,2,1,0:T(8,128)} reshape(f32[256,256]{1,0:T(8,128)} %negate_add_fusion) | data formatting | bytes 524288 | tf_op jit(solution)/shard_map/add | solution.py:98
  59.8 4.0 %reduce_sum.29 = f32[64,64]{1,0:T(8,128)S(1)} reduce(f32[64,4,64,4]{3,2,1,0:T(8,128)} %add.228, f32[]{:T(128)} %constant.9.clone.1), dimensions={1,3}, to_apply=%region_2.3 | reduce | flops 61440 | bytes 278532 | tf_op jit(solution)/shard_map/reduce_sum | solution.py:78
  63.9 6.9 %psum.14 = f32[64,64]{1,0:T(8,128)S(1)} all-reduce(f32[64,64]{1,0:T(8,128)S(1)} %bitcast_multiply_fusion.12), channel_id=1, replica_groups=mesh['member'=16,'slab'=2] {'slab'}, use_global_device_ids=true, to_apply=%region_3.4 | all-reduce | flops 4096 | bytes 32768 | tf_op jit(solution)/shard_map/psum | solution.py:98
  70.8 59.2 %psum.15 = f32[64,64]{1,0:T(8,128)S(1)} all-reduce(f32[64,64]{1,0:T(8,128)S(1)} %psum.14), channel_id=1, replica_groups=mesh['member'=16,'slab'=2] {'member'}, use_global_device_ids=true, to_apply=%region_4.5 | all-reduce | flops 4096 | bytes 32768 | tf_op jit(solution)/shard_map/psum | solution.py:98
  130.0 0.6 broadcast_multiply_fusion
  130.6 1.9 %select_maximum_fusion = f32[2,4,258,258]{3,2,1,0:T(8,128)S(1)} fusion(f32[2,1,256,256]{3,2,1,0:T(8,128)S(1)} %collective-permute-done.4, f32[2,1,256,256]{3,2,1,0:T(8,128)S(1)} %collective-permute-done.5, f32[1,2,256,256]{3,2,1,0:T(8,128)S(1)} %fusion.34, f32[1,2,256,256]{3,2,1,0:T(8,128)S(1)} %get-tuple-element.4), kind=kLoop, calls=%fused_computation.4 | loop fusion | flops 9585216 | bytes 4227200 | tf_op jit(solution)/shard_map/concatenate | solution.py:23
  132.5 0.9 fusion.4
  133.5 0.3 fusion.17
  133.8 1.0 maximum_bitcast_fusion
  (17 shorter events, 0.1 us)
Async XLA Ops:
  0.6 17.5 %copy-start.5 = (f32[64,64]{1,0:T(8,128)S(1)}, f32[64,64]{1,0:T(8,128)}, u32[]{:S(2)}) copy-start(f32[64,64]{1,0:T(8,128)} %param.6) | copy-start | bytes 49156
  0.6 17.5 %copy-start.4 = (f32[1,64,64]{2,1,0:T(8,128)S(1)}, f32[1,64,64]{2,1,0:T(8,128)}, u32[]{:S(2)}) copy-start(f32[1,64,64]{2,1,0:T(8,128)} %param.7) | copy-start | bytes 49156
  2.9 27.5 %collective-permute-start = (f32[2,1,256,256]{3,2,1,0:T(8,128)}, f32[2,1,256,256]{3,2,1,0:T(8,128)S(1)}, u32[]{:S(2)}, u32[]{:S(2)}) collective-permute-start(f32[2,1,256,256]{3,2,1,0:T(8,128)} %get-tuple-element.13), channel_id=1, source_target_pairs={{1,0},{3,2},{5,4},{7,6},{9,8},{11,10},{13,12},{15,14},{17,16},{19,... | collective-permute-start | bytes 1572872 | tf_op jit(solution)/shard_map/ppermute | solution.py:27
  4.2 26.2 %collective-permute-start.1 = (f32[2,1,256,256]{3,2,1,0:T(8,128)}, f32[2,1,256,256]{3,2,1,0:T(8,128)S(1)}, u32[]{:S(2)}, u32[]{:S(2)}) collective-permute-start(f32[2,1,256,256]{3,2,1,0:T(8,128)} %get-tuple-element.12), channel_id=1, source_target_pairs={{0,1},{2,3},{4,5},{6,7},{8,9},{10,11},{12,13},{14,15},{16,17},{18,... | collective-permute-start | bytes 1572872 | tf_op jit(solution)/shard_map/ppermute | solution.py:25
  11.5 24.2 %collective-permute-start.2 = (f32[2,1,256,256]{3,2,1,0:T(8,128)}, f32[2,1,256,256]{3,2,1,0:T(8,128)S(1)}, u32[]{:S(2)}, u32[]{:S(2)}) collective-permute-start(f32[2,1,256,256]{3,2,1,0:T(8,128)} %get-tuple-element.11), channel_id=1, source_target_pairs={{1,0},{3,2},{5,4},{7,6},{9,8},{11,10},{13,12},{15,14},{17,16},{19,... | collective-permute-start | bytes 1572872 | tf_op jit(solution)/shard_map/ppermute | solution.py:27
  12.8 22.9 %collective-permute-start.3 = (f32[2,1,256,256]{3,2,1,0:T(8,128)}, f32[2,1,256,256]{3,2,1,0:T(8,128)}, u32[]{:S(2)}, u32[]{:S(2)}) collective-permute-start(f32[2,1,256,256]{3,2,1,0:T(8,128)} %get-tuple-element.10), channel_id=1, source_target_pairs={{0,1},{2,3},{4,5},{6,7},{8,9},{10,11},{12,13},{14,15},{16,17},{18,... | collective-permute-start | bytes 1572872 | tf_op jit(solution)/shard_map/ppermute | solution.py:25
  22.0 10.0 %copy-start.1 = (f32[1,2,2,256,256]{4,3,2,1,0:T(8,128)S(1)}, f32[1,2,2,256,256]{4,3,2,1,0:T(8,128)}, u32[]{:S(2)}) copy-start(f32[1,2,2,256,256]{4,3,2,1,0:T(8,128)} %param.5) | copy-start | bytes 3145732
  30.4 0.8 copy-start.2
  31.2 0.8 copy-start.3
  33.5 2.3 %copy-start = (f32[1,2,2,256,256]{4,3,2,1,0:T(8,128)S(1)}, f32[1,2,2,256,256]{4,3,2,1,0:T(8,128)}, u32[]{:S(2)}) copy-start(f32[1,2,2,256,256]{4,3,2,1,0:T(8,128)} %param.4) | copy-start | bytes 3145732
  42.3 88.3 %collective-permute-start.4 = (f32[2,1,256,256]{3,2,1,0:T(8,128)}, f32[2,1,256,256]{3,2,1,0:T(8,128)S(1)}, u32[]{:S(2)}, u32[]{:S(2)}) collective-permute-start(f32[2,1,256,256]{3,2,1,0:T(8,128)} %get-tuple-element.9), channel_id=1, source_target_pairs={{1,0},{3,2},{5,4},{7,6},{9,8},{11,10},{13,12},{15,14},{17,16},{19,... | collective-permute-start | bytes 1572872 | tf_op jit(solution)/shard_map/ppermute | solution.py:27
  43.6 87.0 %collective-permute-start.5 = (f32[2,1,256,256]{3,2,1,0:T(8,128)}, f32[2,1,256,256]{3,2,1,0:T(8,128)S(1)}, u32[]{:S(2)}, u32[]{:S(2)}) collective-permute-start(f32[2,1,256,256]{3,2,1,0:T(8,128)} %get-tuple-element.8), channel_id=1, source_target_pairs={{0,1},{2,3},{4,5},{6,7},{8,9},{10,11},{12,13},{14,15},{16,17},{18,... | collective-permute-start | bytes 1572872 | tf_op jit(solution)/shard_map/ppermute | solution.py:25
